TPU v7x, 32 devices: a whole 2x2x4 slice. The times are simulated.
32 devices in a mesh: gz: 2 (over y), row: 4 (over z), col: 4 (over x, core).
Axes of the slice: x: 2, y: 2, z: 4, core: 2. Of those that a mesh axis runs over, the one named last changes fastest.
Arguments:
- lpanel: bfloat16 [2, 2, 1024, 2048], P(None, 'gz', 'row', 'col'), may hold values from -6 to 6
- upanel: bfloat16 [2, 2, 2048, 4096], P(None, 'gz', 'row', 'col'), may hold values from -0.125 to 0.125
- rowmap: int32 [2, 2, 4], P(None, 'gz', 'row'), may hold values from 0 to 1
- colmap: int32 [2, 2, 16], P(None, 'gz', 'col'), may hold values from 0 to 1
- blockmask: int32 [2, 2, 4, 16], P(None, 'gz', 'row', 'col'), may hold values 0 or 1
- front_blocks: bfloat16 [2, 2048, 2048], P(None, 'row', ('gz', 'col')), may hold values from -6 to 6
Outputs:
- front_update: bfloat16 [2, 2048, 2048], P(None, 'row', ('gz', 'col'))
All inputs are finite; a program needn't handle non-finite values. No bound on the sum of `blockmask` on one device may be relied on, other than what follows from the above.
Results may differ from a plain program's by a relative error of at most 0.008.
Values may be sent and summed in bfloat16 or wider, within the bound.
A program may use at most 64 MiB of HBM per device.

v0:
```python
import jax
import jax.numpy as jnp
from jax import lax
from jax.sharding import PartitionSpec as P

CB = 4
FRB = 2
LEVELS = 2


def column_sums(schur, cols_of, live, layers):
    width = schur.shape[0]
    blocks = schur.reshape(width, CB, width)
    targets = cols_of[:, None] == jnp.arange(layers, dtype=jnp.int32)[None, :]
    col_select = targets.astype(jnp.float32) * live.astype(jnp.float32)[:, None]
    return jnp.einsum("bjk,jl->lbk", blocks, col_select, precision=lax.Precision.HIGHEST)


def on_device(lpanel, upanel, rowmap, colmap, blockmask, front_blocks):
    layers = lax.axis_size("gz")
    width = lpanel.shape[2]
    tiles = []
    for depth in range(LEVELS):
        left_rows = lax.all_gather(lpanel[depth, 0], "col", axis=1, tiled=True)
        tiles.append(
            jnp.dot(
                left_rows,
                lax.all_gather(upanel[depth, 0], "row", axis=0, tiled=True),
                preferred_element_type=jnp.float32,
            )
        )
    results = []
    every_row = lax.all_gather(rowmap[:, :, 0], "gz", axis=1, tiled=True)
    for depth in range(LEVELS):
        sums = column_sums(tiles[depth], colmap[depth, 0], blockmask[depth, 0, 0], layers).astype(
            jnp.bfloat16
        )
        arrived = lax.all_to_all(sums, "gz", split_axis=0, concat_axis=0, tiled=True)
        row_select = (
            every_row[depth][:, None] == jnp.arange(FRB, dtype=jnp.int32)[None, :]
        ).astype(jnp.float32)
        placed = jnp.einsum(
            "sf,sbk->fbk", row_select, arrived.astype(jnp.float32), precision=lax.Precision.HIGHEST
        )
        placed = placed.reshape(FRB * width, width)
        results.append((front_blocks[depth].astype(jnp.float32) - placed).astype(jnp.bfloat16))
    return jnp.stack(results)


def solution(mesh):
    return jax.shard_map(
        on_device,
        mesh=mesh,
        in_specs=(
            P(None, "gz", "row", "col"),
            P(None, "gz", "row", "col"),
            P(None, "gz", "row"),
            P(None, "gz", "col"),
            P(None, "gz", "row", "col"),
            P(None, "row", ("gz", "col")),
        ),
        out_specs=P(None, "row", ("gz", "col")),
        check_vma=False,
    )
```

profile of v0, /device:TPU:0, one launch (start us, length us, event | category | flops | bytes accessed | tf_op | source)
XLA Modules:
  0.0 233.3 jit_solution(11607973577861634287)
XLA Ops:
  6.5 1.9 fusion.31
  8.5 3.0 %fusion.30 = (bf16[1,1,512,1024]{3,2,1,0:T(8,128)(2,1)}, bf16[1,1,512,1024]{3,2,1,0:T(8,128)(2,1)}) fusion(bf16[2,1,512,1024]{3,2,1,0:T(8,128)(2,1)} %param.7), kind=kLoop, calls=%fused_computation.43 | loop fusion | bytes 4194304 | tf_op jit(solution)/shard_map/slice | solution.py:28
  11.7 0.7 all-gather.10.cloned.1.call-update
  12.4 0.5 all-gather.12.cloned.1.call-update
  12.9 5.2 %all-gather = s32[2,2,1]{0,2,1:T(1,128)S(1)} all-gather(s32[2,1,1]{0,2,1:T(1,128)S(1)} %copy-done.4), channel_id=2, replica_groups=mesh['gz'=2,'row'=4,'col'=4] {'gz'}, dimensions={1}, use_global_device_ids=true | all-gather | bytes 24 | tf_op jit(solution)/shard_map/all_gather | solution.py:33
  18.1 0.2 slice_reduce_fusion.1
  18.4 10.0 %all-gather.14.cloned.1.call-done = bf16[1,1,256,2048]{3,2,1,0:T(8,128)(2,1)} async-done(((bf16[1,1,256,512]{3,2,1,0:T(8,128)(2,1)}), bf16[1,1,256,2048]{3,2,1,0:T(8,128)(2,1)}) %all-gather.14.cloned.1.call-update) | async-done | bytes 1048592 | tf_op jit(solution)/shard_map/all_gather | solution.py:24
  28.4 82.3 %all-gather.16.cloned.1.call-done = bf16[1,1,2048,1024]{3,2,1,0:T(8,128)(2,1)} async-done(((bf16[1,1,512,1024]{3,2,1,0:T(8,128)(2,1)}), bf16[1,1,2048,1024]{3,2,1,0:T(8,128)(2,1)}) %all-gather.16.cloned.1.call-update) | async-done | bytes 4194320 | tf_op jit(solution)/shard_map/all_gather | solution.py:28
  110.7 3.8 %fusion = f32[256,1024]{1,0:T(8,128)S(1)} fusion(bf16[1,1,2048,1024]{3,2,1,0:T(8,128)(2,1)} %all-gather.16.cloned.1.call-done, bf16[1,1,256,2048]{3,2,1,0:T(8,128)(2,1)} %all-gather.14.cloned.1.call-done), kind=kOutput, calls=%fused_computation | convolution fusion | flops 1073741824 | bytes 6291456 | tf_op jit(solution)/shard_map/dot_general | solution.py:26
  114.5 0.5 reshape.32
  115.0 1.9 convolution_convert_fusion
  116.8 0.8 copy.12
  117.6 3.4 %all-to-all-start.1 = ((bf16[2,256,256]{2,1,0:T(8,128)(2,1)}), bf16[2,256,256]{2,1,0:T(8,128)(2,1)S(1)}, u32[]{:S(2)}, u32[]{:S(2)}) async-start(bf16[2,256,256]{2,1,0:T(8,128)(2,1)} %copy.12), calls=%async_computation.1 | async-start | bytes 524288 | tf_op jit(solution)/shard_map/all_to_all | solution.py:38
  121.0 6.4 %all-gather.10.cloned.1.call-done = bf16[1,1,256,2048]{3,2,1,0:T(8,128)(2,1)} async-done(((bf16[1,1,256,512]{3,2,1,0:T(8,128)(2,1)}), bf16[1,1,256,2048]{3,2,1,0:T(8,128)(2,1)}) %all-gather.10.cloned.1.call-update) | async-done | bytes 1048592 | tf_op jit(solution)/shard_map/all_gather | solution.py:24
  127.5 82.2 %all-gather.12.cloned.1.call-done = bf16[1,1,2048,1024]{3,2,1,0:T(8,128)(2,1)} async-done(((bf16[1,1,512,1024]{3,2,1,0:T(8,128)(2,1)}), bf16[1,1,2048,1024]{3,2,1,0:T(8,128)(2,1)}) %all-gather.12.cloned.1.call-update) | async-done | bytes 4194320 | tf_op jit(solution)/shard_map/all_gather | solution.py:28
  209.7 3.8 %fusion.2 = f32[256,1024]{1,0:T(8,128)S(1)} fusion(bf16[1,1,2048,1024]{3,2,1,0:T(8,128)(2,1)} %all-gather.12.cloned.1.call-done, bf16[1,1,256,2048]{3,2,1,0:T(8,128)(2,1)} %all-gather.10.cloned.1.call-done), kind=kOutput, calls=%fused_computation.2 | convolution fusion | flops 1073741824 | bytes 6291456 | tf_op jit(solution)/shard_map/dot_general | solution.py:26
  213.5 0.5 reshape.30
  214.0 1.9 convolution_convert_fusion.1
  215.8 0.7 copy.9
  216.6 3.4 %all-to-all-start = ((bf16[2,256,256]{2,1,0:T(8,128)(2,1)}), bf16[2,256,256]{2,1,0:T(8,128)(2,1)S(1)}, u32[]{:S(2)}, u32[]{:S(2)}) async-start(bf16[2,256,256]{2,1,0:T(8,128)(2,1)} %copy.9), calls=%async_computation | async-start | bytes 524288 | tf_op jit(solution)/shard_map/all_to_all | solution.py:38
  220.0 0.4 fusion.8
  220.5 4.8 %all-to-all-done = bf16[2,256,256]{2,1,0:T(8,128)(2,1)S(1)} async-done(((bf16[2,256,256]{2,1,0:T(8,128)(2,1)}), bf16[2,256,256]{2,1,0:T(8,128)(2,1)S(1)}, u32[]{:S(2)}, u32[]{:S(2)}) %all-to-all-start) | async-done | bytes 262176 | tf_op jit(solution)/shard_map/all_to_all | solution.py:38
  225.3 0.4 fusion.10
  225.9 0.8 copy-done.3
  (22 shorter events, 0.4 us)
Async XLA Ops:
  6.5 6.4 %copy-start.4 = (s32[2,1,1]{0,2,1:T(1,128)S(1)}, s32[2,1,1]{0,2,1:T(1,128)}, u32[]{:S(2)}) copy-start(s32[2,1,1]{0,2,1:T(1,128)} %param.8) | copy-start | bytes 28
  6.5 11.8 %copy-start.1 = (s32[2,1,4]{2,1,0:T(1,128)S(1)}, s32[2,1,4]{2,1,0:T(1,128)}, u32[]{:S(2)}) copy-start(s32[2,1,4]{2,1,0:T(1,128)} %param.9) | copy-start | bytes 100
  6.5 11.8 %copy-start.2 = (s32[2,1,1,4]{3,2,1,0:T(1,128)S(1)}, s32[2,1,1,4]{3,2,1,0:T(1,128)}, u32[]{:S(2)}) copy-start(s32[2,1,1,4]{3,2,1,0:T(1,128)} %param.10) | copy-start | bytes 100
  6.5 21.8 %all-gather.14.cloned.1.call-start = ((), (), s32[]{:S(2)}) async-start(), calls=%async_computation.4 | async-start | bytes 1310720 | tf_op jit(solution)/shard_map/all_gather | solution.py:24
  8.5 102.2 %all-gather.16.cloned.1.call-start = ((), (), s32[]{:S(2)}) async-start(), calls=%async_computation.5 | async-start | bytes 5242880 | tf_op jit(solution)/shard_map/all_gather | solution.py:28
  11.6 115.9 %all-gather.10.cloned.1.call-start = ((), (), s32[]{:S(2)}) async-start(), calls=%async_computation.2 | async-start | bytes 1310720 | tf_op jit(solution)/shard_map/all_gather | solution.py:24
  12.3 197.3 %all-gather.12.cloned.1.call-start = ((), (), s32[]{:S(2)}) async-start(), calls=%async_computation.3 | async-start | bytes 5242880 | tf_op jit(solution)/shard_map/all_gather | solution.py:28
  117.6 99.0 %all-to-all-start.1 = ((bf16[2,256,256]{2,1,0:T(8,128)(2,1)}), bf16[2,256,256]{2,1,0:T(8,128)(2,1)S(1)}, u32[]{:S(2)}, u32[]{:S(2)}) async-start(bf16[2,256,256]{2,1,0:T(8,128)(2,1)} %copy.12), calls=%async_computation.1 | async-start | bytes 524288 | tf_op jit(solution)/shard_map/all_to_all | solution.py:38
  213.4 12.3 %copy-start = (bf16[2,512,256]{2,1,0:T(8,128)(2,1)S(1)}, bf16[2,512,256]{2,1,0:T(8,128)(2,1)}, u32[]{:S(2)}) copy-start(bf16[2,512,256]{2,1,0:T(8,128)(2,1)} %param.11) | copy-start | bytes 1572868
  216.6 8.7 %all-to-all-start = ((bf16[2,256,256]{2,1,0:T(8,128)(2,1)}), bf16[2,256,256]{2,1,0:T(8,128)(2,1)S(1)}, u32[]{:S(2)}, u32[]{:S(2)}) async-start(bf16[2,256,256]{2,1,0:T(8,128)(2,1)} %copy.9), calls=%async_computation | async-start | bytes 524288 | tf_op jit(solution)/shard_map/all_to_all | solution.py:38
  225.9 0.8 copy-start.3
Sparse Core Ops, SparseCore 0:
  8.9 19.4 all-gather.13
  29.9 80.7 all-gather.15
  112.3 15.1 all-gather.9
  128.9 80.7 all-gather.11
where the time goes:
time: 234 us; the launch traced here: 233 us
  waiting for transfers between devices  187 us (80%)
  between operations  13.3 us (6%)
  matrix products  12.1 us (5%)
  local copies, waits for them, and re-layouts  8.54 us (4%)
  starting transfers between devices  7.01 us (3%)
  blocking collectives  5.19 us (2%)
    all_gather x2, waiting for transfers between devices, on_device(): lax.all_gather(upanel[depth, 0], 'row', axis=0, tiled=True)  165 us
    all_gather x2, waiting for transfers between devices, on_device(): left_rows = lax.all_gather(lpanel[depth, 0], 'col', axis=1, tiled=True)  16.4 us
    dot_general x2, matrix products, on_device(): jnp.dot(left_rows, lax.all_gather(upanel[depth, 0], 'row', axis=0, tiled=...  7.52 us
    all_to_all x2, starting transfers between devices, on_device(): lax.all_to_all(sums, 'gz', split_axis=0, concat_axis=0, tiled=True)  6.89 us
    all_gather x1, blocking collectives, on_device(): every_row = lax.all_gather(rowmap[:, :, 0], 'gz', axis=1, tiled=True)  5.19 us
    all_to_all x2, waiting for transfers between devices, on_device(): lax.all_to_all(sums, 'gz', split_axis=0, concat_axis=0, tiled=True)  4.82 us
  transfers between devices with their start and end apart: 6, of which 5 were waited for; matrix products, arithmetic and copies ran while one was open for 7% of the time, Pallas kernels for 0%

commit v1 on v0

--- a/solution.py
+++ b/solution.py
@@ -1,11 +1,15 @@
+import functools
+
 import jax
 import jax.numpy as jnp
 from jax import lax
+from jax.experimental import pallas as pl
+from jax.experimental.pallas import tpu as pltpu
 from jax.sharding import PartitionSpec as P
 
 CB = 4
 FRB = 2
-LEVELS = 2
+MESH = pl.DeviceIdType.MESH
 
 
 def column_sums(schur, cols_of, live, layers):
@@ -16,11 +20,12 @@
     return jnp.einsum("bjk,jl->lbk", blocks, col_select, precision=lax.Precision.HIGHEST)
 
 
-def on_device(lpanel, upanel, rowmap, colmap, blockmask, front_blocks):
+def general(lpanel, upanel, rowmap, colmap, blockmask, front_blocks):
     layers = lax.axis_size("gz")
     width = lpanel.shape[2]
+    levels = lpanel.shape[0]
     tiles = []
-    for depth in range(LEVELS):
+    for depth in range(levels):
         left_rows = lax.all_gather(lpanel[depth, 0], "col", axis=1, tiled=True)
         tiles.append(
             jnp.dot(
@@ -31,7 +36,7 @@
         )
     results = []
     every_row = lax.all_gather(rowmap[:, :, 0], "gz", axis=1, tiled=True)
-    for depth in range(LEVELS):
+    for depth in range(levels):
         sums = column_sums(tiles[depth], colmap[depth, 0], blockmask[depth, 0, 0], layers).astype(
             jnp.bfloat16
         )
@@ -47,9 +52,275 @@
     return jnp.stack(results)
 
 
+def kernel(
+    rows, cols, layers, levels, width,
+    l_ref, u_hbm, coef_ref, rm_ref, front_hbm, out_ref,
+    u_ref, front_ref, crossed, l_all, coef_all, own, part, p_in, y_out, y_in, rm_in,
+    in_sem, x_send, x_recv, l_send, l_recv, loc_sem, relay_send, m_send, m_recv, m_loc,
+    p_send, p_recv, y_send, y_recv, rm_send, rm_recv,
+):
+    z = lax.axis_index("row")
+    c = lax.axis_index("col")
+    g = lax.axis_index("gz")
+    far = lax.rem(c + cols // 2, cols)
+    mate = c + 1 - 2 * lax.rem(c, 2)
+    other = 1 - g
+    gate = lax.rem(c, 2) == lax.rem(z, 2)
+
+    loads = [pltpu.make_async_copy(u_hbm.at[v], u_ref.at[v], in_sem.at[v]) for v in range(levels)]
+    loads.append(pltpu.make_async_copy(front_hbm, front_ref, in_sem.at[levels]))
+    for load in loads:
+        load.start()
+
+    barrier = pltpu.get_barrier_semaphore()
+    for step in range(1, rows):
+        pl.semaphore_signal(
+            barrier, inc=1, device_id={"row": lax.rem(z + step, rows)}, device_id_type=MESH
+        )
+    pl.semaphore_signal(barrier, inc=1, device_id={"col": far}, device_id_type=MESH)
+    pl.semaphore_signal(barrier, inc=1, device_id={"col": mate}, device_id_type=MESH)
+    pl.semaphore_signal(barrier, inc=1, device_id={"gz": other}, device_id_type=MESH)
+    pl.semaphore_wait(barrier, rows + 2)
+
+    def remote(src, dst, send, recv, where):
+        return pltpu.make_async_remote_copy(
+            src_ref=src, dst_ref=dst, send_sem=send, recv_sem=recv,
+            device_id=where, device_id_type=MESH,
+        )
+
+    own_coef = pltpu.make_async_copy(coef_ref, coef_all.at[z], m_loc)
+    own_coef.start()
+    coef_out = []
+    for step in range(1, rows):
+        to = lax.rem(z + step, rows)
+        coef_out.append(
+            remote(coef_ref, coef_all.at[z], m_send.at[step], m_recv.at[z], {"row": to})
+        )
+        coef_out[-1].start()
+    rm_copy = remote(rm_ref, rm_in, rm_send, rm_recv, {"gz": other})
+    rm_copy.start()
+
+    across = [
+        remote(l_ref.at[v], crossed.at[v], x_send.at[v], x_recv.at[v], {"col": far})
+        for v in range(levels)
+    ]
+
+    def place(v, half):
+        k = c if half == 0 else far
+        block = l_ref.at[v] if half == 0 else crossed.at[v]
+        copy = remote(block, l_all.at[v, z], l_send.at[v, half], l_recv.at[v, z], {"row": k})
+        local = pltpu.make_async_copy(block, l_all.at[v, z], loc_sem.at[v])
+        return k, copy, local
+
+    def start_place(v, half):
+        k, copy, local = place(v, half)
+
+        @pl.when(k != z)
+        def _():
+            copy.start()
+
+        @pl.when(k == z)
+        def _():
+            local.start()
+
+    for v in range(levels):
+        across[v].start()
+    start_place(0, 0)
+    across[0].wait_recv()
+    start_place(0, 1)
+    for v in range(1, levels):
+        start_place(v, 0)
+        across[v].wait_recv()
+        start_place(v, 1)
+
+    own_coef.wait()
+    for step in range(1, rows):
+        src = lax.rem(z + step, rows)
+        remote(coef_ref, coef_all.at[src], m_send.at[step], m_recv.at[src], {"row": src}).wait_recv()
+
+    def item(v, i):
+        odd = lax.rem(i, 2)
+        a = (1 - odd) * (rows - 1 - i // 2) + odd * (i // 2)
+        relay = remote(
+            l_all.at[v, a], l_all.at[v, a], relay_send.at[v, a], l_recv.at[v, a], {"col": mate}
+        )
+
+        @pl.when(gate)
+        def _():
+            @pl.when(a == z)
+            def _():
+                pltpu.make_async_copy(l_ref.at[v], l_all.at[v, z], loc_sem.at[v]).wait()
+
+            @pl.when(a != z)
+            def _():
+                relay.wait_recv()
+
+            relay.start()
+
+        @pl.when(jnp.logical_not(gate))
+        def _():
+            relay.wait_recv()
+
+        left = l_all[v, a]
+        for j in range(CB):
+            lanes = slice(j * width, (j + 1) * width)
+            t = jnp.dot(left, u_ref[v, :, lanes], preferred_element_type=jnp.float32)
+            for l in range(layers):
+                m = coef_all[a, pl.ds(v * layers + l, 1), lanes]
+                if j == 0:
+                    own[v, l] = t * m
+                else:
+                    own[v, l] += t * m
+
+        def send(side, to):
+            for l in range(layers):
+                part[v, a, l] = own[v, l].astype(jnp.bfloat16)
+            remote(
+                part.at[v, a], p_in.at[v, side, a], p_send.at[v, a], p_recv.at[v, side, a], {"row": to}
+            ).start()
+
+        def forward(side, to, has_up):
+            @pl.when(has_up)
+            def _():
+                remote(
+                    part.at[v, a], p_in.at[v, side, a], p_send.at[v, a], p_recv.at[v, side, a], {"row": to}
+                ).wait_recv()
+                for l in range(layers):
+                    own[v, l] += p_in[v, side, a, l].astype(jnp.float32)
+
+            send(side, to)
+
+        @pl.when(a > z)
+        def _():
+            forward(0, lax.rem(z + 1, rows), z > 0)
+
+        @pl.when(a < z)
+        def _():
+            forward(1, lax.rem(z + rows - 1, rows), z < rows - 1)
+
+        @pl.when(a == z)
+        def _():
+            for l in range(layers):
+                own[levels + v, l] = own[v, l]
+
+    def run(v):
+        def body(i, carry):
+            item(v, i)
+            return carry
+
+        lax.fori_loop(0, rows, body, 0)
+
+    for v in range(levels):
+        loads[v].wait()
+        run(v)
+
+    ways = []
+    for v in range(levels):
+        for side, there in ((0, z > 0), (1, z < rows - 1)):
+            @pl.when(there)
+            def _(side=side):
+                remote(
+                    part.at[v, z], p_in.at[v, side, z], p_send.at[v, z], p_recv.at[v, side, z], {"gz": other}
+                ).wait_recv()
+                for l in range(layers):
+                    own[levels + v, l] += p_in[v, side, z, l].astype(jnp.float32)
+
+        y_out[v] = own[levels + v, other].astype(jnp.bfloat16)
+        way = remote(y_out.at[v], y_in.at[v], y_send.at[v], y_recv.at[v], {"gz": other})
+        way.start()
+        ways.append(way)
+
+    loads[levels].wait()
+    rm_copy.wait()
+    for v in range(levels):
+        mine = own[levels + v, g].astype(jnp.bfloat16).astype(jnp.float32)
+        ways[v].wait_recv()
+        theirs = y_in[v].astype(jnp.float32)
+        for f in range(FRB):
+            lines = slice(f * width, (f + 1) * width)
+            here = (rm_ref[v : v + 1, :] == f).astype(jnp.float32)
+            away = (rm_in[v : v + 1, :] == f).astype(jnp.float32)
+            total = here * mine + away * theirs
+            out_ref[v, lines, :] = (front_ref[v, lines, :].astype(jnp.float32) - total).astype(
+                out_ref.dtype
+            )
+
+    for copy in coef_out:
+        copy.wait_send()
+    for v in range(levels):
+        across[v].wait_send()
+        ways[v].wait_send()
+        for half in range(2):
+            k, copy, _local = place(v, half)
+            pl.when(k != z)(copy.wait_send)
+        for a in range(rows):
+            relay = remote(
+                l_all.at[v, a], l_all.at[v, a], relay_send.at[v, a], l_recv.at[v, a], {"col": mate}
+            )
+            pl.when(gate)(relay.wait_send)
+            sent = remote(
+                part.at[v, a], p_in.at[v, 0, a], p_send.at[v, a], p_recv.at[v, 0, a], {"gz": other}
+            )
+            pl.when(a != z)(sent.wait_send)
+
+
+def stationary(rows, cols, layers, lpanel, upanel, rowmap, colmap, blockmask, front_blocks):
+    levels, _, width, depth = lpanel.shape
+    wide = upanel.shape[3]
+    select = colmap[:, 0, None, :] == jnp.arange(layers, dtype=jnp.int32)[None, :, None]
+    coef = select.astype(jnp.float32) * blockmask[:, 0, 0, None, :].astype(jnp.float32)
+    coef = jnp.broadcast_to(coef[..., None], (levels, layers, CB, width))
+    coef = coef.reshape(levels * layers, wide)
+    rm = jnp.broadcast_to(rowmap[:, 0], (levels, width))
+    bf16 = jnp.bfloat16
+    vmem = pl.BlockSpec(memory_space=pltpu.VMEM)
+    hbm = pl.BlockSpec(memory_space=pl.ANY)
+    dma = pltpu.SemaphoreType.DMA
+    return pl.pallas_call(
+        functools.partial(kernel, rows, cols, layers, levels, width),
+        out_shape=jax.ShapeDtypeStruct(front_blocks.shape, front_blocks.dtype),
+        in_specs=[vmem, hbm, vmem, vmem, hbm],
+        out_specs=vmem,
+        scratch_shapes=[
+            pltpu.VMEM(upanel[:, 0].shape, bf16),
+            pltpu.VMEM(front_blocks.shape, bf16),
+            pltpu.VMEM((levels, width, depth), bf16),
+            pltpu.VMEM((levels, rows, width, depth), bf16),
+            pltpu.VMEM((rows, levels * layers, wide), jnp.float32),
+            pltpu.VMEM((2 * levels, layers, width, width), jnp.float32),
+            pltpu.VMEM((levels, rows, layers, width, width), bf16),
+            pltpu.VMEM((levels, 2, rows, layers, width, width), bf16),
+            pltpu.VMEM((levels, width, width), bf16),
+            pltpu.VMEM((levels, width, width), bf16),
+            pltpu.VMEM((levels, width), jnp.int32),
+            dma((levels + 1,)),
+            dma((levels,)),
+            dma((levels,)),
+            dma((levels, 2)),
+            dma((levels, rows)),
+            dma((levels,)),
+            dma((levels, rows)),
+            dma((rows,)),
+            dma((rows,)),
+            dma,
+            dma((levels, rows)),
+            dma((levels, 2, rows)),
+            dma((levels,)),
+            dma((levels,)),
+            dma,
+            dma,
+        ],
+        compiler_params=pltpu.CompilerParams(collective_id=0, has_side_effects=True),
+    )(lpanel[:, 0], upanel[:, 0], coef, rm, front_blocks)
+
+
 def solution(mesh):
+    rows, cols, layers = mesh.shape["row"], mesh.shape["col"], mesh.shape["gz"]
+    body = general
+    if rows == cols == 2 * layers and layers == 2:
+        body = functools.partial(stationary, rows, cols, layers)
     return jax.shard_map(
-        on_device,
+        body,
         mesh=mesh,
         in_specs=(
             P(None, "gz", "row", "col"),

time: 234 us -> 93.4 us (0.40)
  waiting for transfers between devices: 187 us -> 0 us
  Pallas kernels: 0 us -> 87.9 us
  between operations: 13.3 us -> 0.01 us
  matrix products: 12.1 us -> 0 us
  starting transfers between devices: 7.01 us -> 0 us
  blocking collectives: 5.19 us -> 0 us
  local copies, waits for them, and re-layouts: 8.54 us -> 3.87 us
    all_gather x4 -> x0, waiting for transfers between devices: 181 us -> none  [the longest x2 165 us: on_device(): lax.all_gather(upanel[depth, 0], 'row', axis=0, tiled=True)]
    pallas_call x0 -> x1, Pallas kernels: none -> 87.9 us  [stationary(): pl.pallas_call(functools.partial(kernel, rows, cols, layers, levels, widt...]
    dot_general x6 -> x0, matrix products: 12.1 us -> none  [the longest x2 7.52 us: on_device(): jnp.dot(left_rows, lax.all_gather(upanel[depth, 0], 'row', axis=0, tiled=...]
    all_to_all x2 -> x0, starting transfers between devices: 6.89 us -> none  [on_device(): lax.all_to_all(sums, 'gz', split_axis=0, concat_axis=0, tiled=True)]
    all_gather x1 -> x0, blocking collectives: 5.19 us -> none  [on_device(): every_row = lax.all_gather(rowmap[:, :, 0], 'gz', axis=1, tiled=True)]
    slice x3 -> x0, local copies, waits for them, and re-layouts: 5.19 us -> none  [the longest x1 3.05 us: on_device(): upanel[depth, 0]]
    all_to_all x2 -> x0, waiting for transfers between devices: 4.82 us -> none  [on_device(): lax.all_to_all(sums, 'gz', split_axis=0, concat_axis=0, tiled=True)]
  transfers between devices with their start and end apart: 6 -> 0, of which waited for: 5 -> 0; matrix products, arithmetic and copies ran while one was open for 7% -> 0% of each run, Pallas kernels for 0% -> 0%
where the time goes in v1:
time: 93.4 us; the launch traced here: 93.2 us
  Pallas kernels  87.9 us (94%)
  local copies, waits for them, and re-layouts  3.87 us (4%)
  other arithmetic  1.36 us (1%)
    pallas_call x1, Pallas kernels, stationary(): pl.pallas_call(functools.partial(kernel, rows, cols, layers, levels, widt...  87.9 us
    unnamed x2, local copies, waits for them, and re-layouts  2.48 us

profile of v1, /device:TPU:0, one launch (start us, length us, event | category | flops | bytes accessed | tf_op | source)
XLA Modules:
  0.0 93.2 jit_solution(173772448103943984)
XLA Ops:
  0.0 0.7 convert_element_type.12
  0.7 0.7 compare_select_fusion
  1.4 1.3 %broadcast_in_dim.16.rm_ref = s32[2,256]{1,0:T(2,128)} broadcast(s32[2]{0:T(128)} %bitcast.14), dimensions={0} | broadcast | bytes 2056 | tf_op jit(solution)/shard_map/broadcast_in_dim | solution.py:274
  2.7 0.1 broadcast_in_dim.6
  2.8 0.6 copy.7
  3.4 87.9 %shard_map.64 = bf16[2,512,256]{2,1,0:T(8,128)(2,1)} custom-call(bf16[2,256,512]{2,1,0:T(8,128)(2,1)} %bitcast.9, bf16[2,512,1024]{2,1,0:T(8,128)(2,1)} %bitcast.8, f32[4,1024]{1,0:T(4,128)} %bitcast.10, s32[2,256]{1,0:T(2,128)} %broadcast_in_dim.16.rm_ref, bf16[2,512,256]{2,1,0:T(8,128)(2,1)} %front_hbm.1), custom_call_target="tpu_custom_call" | custom-call | tf_op jit(solution)/shard_map/pallas_call | solution.py:279
  91.3 1.9 %copy.9 = bf16[2,512,256]{2,1,0:T(8,128)(2,1)} copy(bf16[2,512,256]{2,1,0:T(8,128)(2,1)} %shard_map.64) | data formatting | bytes 1048576

commit v2 on v1

--- a/solution.py
+++ b/solution.py
@@ -54,8 +54,8 @@
 
 def kernel(
     rows, cols, layers, levels, width,
-    l_ref, u_hbm, coef_ref, rm_ref, front_hbm, out_ref,
-    u_ref, front_ref, crossed, l_all, coef_all, own, part, p_in, y_out, y_in, rm_in,
+    l_hbm, u_hbm, cm_ref, live_ref, rm_ref, front_hbm, out_ref,
+    l_ref, u_ref, front_ref, crossed, l_all, live_all, own, part, p_in, y_out, y_in, rm_in,
     in_sem, x_send, x_recv, l_send, l_recv, loc_sem, relay_send, m_send, m_recv, m_loc,
     p_send, p_recv, y_send, y_recv, rm_send, rm_recv,
 ):
@@ -69,6 +69,8 @@
 
     loads = [pltpu.make_async_copy(u_hbm.at[v], u_ref.at[v], in_sem.at[v]) for v in range(levels)]
     loads.append(pltpu.make_async_copy(front_hbm, front_ref, in_sem.at[levels]))
+    first = pltpu.make_async_copy(l_hbm, l_ref, in_sem.at[levels + 1])
+    first.start()
     for load in loads:
         load.start()
 
@@ -87,18 +89,6 @@
             src_ref=src, dst_ref=dst, send_sem=send, recv_sem=recv,
             device_id=where, device_id_type=MESH,
         )
-
-    own_coef = pltpu.make_async_copy(coef_ref, coef_all.at[z], m_loc)
-    own_coef.start()
-    coef_out = []
-    for step in range(1, rows):
-        to = lax.rem(z + step, rows)
-        coef_out.append(
-            remote(coef_ref, coef_all.at[z], m_send.at[step], m_recv.at[z], {"row": to})
-        )
-        coef_out[-1].start()
-    rm_copy = remote(rm_ref, rm_in, rm_send, rm_recv, {"gz": other})
-    rm_copy.start()
 
     across = [
         remote(l_ref.at[v], crossed.at[v], x_send.at[v], x_recv.at[v], {"col": far})
@@ -123,9 +113,23 @@
         def _():
             local.start()
 
+    first.wait()
     for v in range(levels):
         across[v].start()
     start_place(0, 0)
+
+    own_live = pltpu.make_async_copy(live_ref, live_all.at[z], m_loc)
+    own_live.start()
+    live_out = []
+    for step in range(1, rows):
+        to = lax.rem(z + step, rows)
+        live_out.append(
+            remote(live_ref, live_all.at[z], m_send.at[step], m_recv.at[z], {"row": to})
+        )
+        live_out[-1].start()
+    rm_copy = remote(rm_ref, rm_in, rm_send, rm_recv, {"gz": other})
+    rm_copy.start()
+
     across[0].wait_recv()
     start_place(0, 1)
     for v in range(1, levels):
@@ -133,14 +137,32 @@
         across[v].wait_recv()
         start_place(v, 1)
 
-    own_coef.wait()
+    own_live.wait()
     for step in range(1, rows):
         src = lax.rem(z + step, rows)
-        remote(coef_ref, coef_all.at[src], m_send.at[step], m_recv.at[src], {"row": src}).wait_recv()
-
-    def item(v, i):
-        odd = lax.rem(i, 2)
-        a = (1 - odd) * (rows - 1 - i // 2) + odd * (i // 2)
+        remote(live_ref, live_all.at[src], m_send.at[step], m_recv.at[src], {"row": src}).wait_recv()
+
+    low = 1 - z // (rows // 2)
+
+    def order(i):
+        near = jnp.int32(i) if isinstance(i, int) else i
+        wrap = near // (rows // 2)
+        up = rows - 1 - near + wrap * (2 * near - rows - rows // 2 + 1)
+        return low * up + (1 - low) * (rows - 1 - up)
+
+    def hop(v, a, side, to):
+        return remote(
+            part.at[v, a], p_in.at[v, side, a], p_send.at[v, a], p_recv.at[v, side, a], {"row": to}
+        )
+
+    right, left = lax.rem(z + 1, rows), lax.rem(z + rows - 1, rows)
+
+    def send(v, a, side, to):
+        for l in range(layers):
+            part[v, a, l] = own[v, a, l].astype(jnp.bfloat16)
+        hop(v, a, side, to).start()
+
+    def item(v, a):
         relay = remote(
             l_all.at[v, a], l_all.at[v, a], relay_send.at[v, a], l_recv.at[v, a], {"col": mate}
         )
@@ -161,71 +183,68 @@
         def _():
             relay.wait_recv()
 
-        left = l_all[v, a]
+        block = l_all[v, a]
         for j in range(CB):
-            lanes = slice(j * width, (j + 1) * width)
-            t = jnp.dot(left, u_ref[v, :, lanes], preferred_element_type=jnp.float32)
+            t = jnp.dot(
+                block, u_ref[v, :, j * width : (j + 1) * width], preferred_element_type=jnp.float32
+            )
+            to_layer = cm_ref[v : v + 1, j : j + 1]
+            live = live_all[a, v : v + 1, j : j + 1]
             for l in range(layers):
-                m = coef_all[a, pl.ds(v * layers + l, 1), lanes]
+                m = jnp.where(to_layer == l, live, 0).astype(jnp.float32)
                 if j == 0:
-                    own[v, l] = t * m
+                    own[v, a, l] = t * m
                 else:
-                    own[v, l] += t * m
-
-        def send(side, to):
-            for l in range(layers):
-                part[v, a, l] = own[v, l].astype(jnp.bfloat16)
-            remote(
-                part.at[v, a], p_in.at[v, side, a], p_send.at[v, a], p_recv.at[v, side, a], {"row": to}
-            ).start()
-
-        def forward(side, to, has_up):
-            @pl.when(has_up)
-            def _():
-                remote(
-                    part.at[v, a], p_in.at[v, side, a], p_send.at[v, a], p_recv.at[v, side, a], {"row": to}
-                ).wait_recv()
-                for l in range(layers):
-                    own[v, l] += p_in[v, side, a, l].astype(jnp.float32)
-
-            send(side, to)
-
-        @pl.when(a > z)
-        def _():
-            forward(0, lax.rem(z + 1, rows), z > 0)
-
-        @pl.when(a < z)
-        def _():
-            forward(1, lax.rem(z + rows - 1, rows), z < rows - 1)
-
-        @pl.when(a == z)
-        def _():
-            for l in range(layers):
-                own[levels + v, l] = own[v, l]
-
-    def run(v):
+                    own[v, a, l] += t * m
+
+        @pl.when(jnp.logical_and(a > z, z == 0))
+        def _():
+            send(v, a, 0, right)
+
+        @pl.when(jnp.logical_and(a < z, z == rows - 1))
+        def _():
+            send(v, a, 1, left)
+
+    def collect(v, a, side):
+        hop(v, a, side, right).wait_recv()
+        for l in range(layers):
+            own[v, a, l] += p_in[v, side, a, l].astype(jnp.float32)
+
+    def forward(v, a):
+        @pl.when(jnp.logical_and(a > z, z > 0))
+        def _():
+            collect(v, a, 0)
+            send(v, a, 0, right)
+
+        @pl.when(jnp.logical_and(a < z, z < rows - 1))
+        def _():
+            collect(v, a, 1)
+            send(v, a, 1, left)
+
+    def over_rows(step, v):
         def body(i, carry):
-            item(v, i)
+            step(v, order(i))
             return carry
 
         lax.fori_loop(0, rows, body, 0)
 
     for v in range(levels):
         loads[v].wait()
-        run(v)
+        over_rows(item, v)
 
     ways = []
     for v in range(levels):
-        for side, there in ((0, z > 0), (1, z < rows - 1)):
-            @pl.when(there)
-            def _(side=side):
-                remote(
-                    part.at[v, z], p_in.at[v, side, z], p_send.at[v, z], p_recv.at[v, side, z], {"gz": other}
-                ).wait_recv()
-                for l in range(layers):
-                    own[levels + v, l] += p_in[v, side, z, l].astype(jnp.float32)
-
-        y_out[v] = own[levels + v, other].astype(jnp.bfloat16)
+        over_rows(forward, v)
+
+        @pl.when(z > 0)
+        def _():
+            collect(v, z, 0)
+
+        @pl.when(z < rows - 1)
+        def _():
+            collect(v, z, 1)
+
+        y_out[v] = own[v, z, other].astype(jnp.bfloat16)
         way = remote(y_out.at[v], y_in.at[v], y_send.at[v], y_recv.at[v], {"gz": other})
         way.start()
         ways.append(way)
@@ -233,7 +252,7 @@
     loads[levels].wait()
     rm_copy.wait()
     for v in range(levels):
-        mine = own[levels + v, g].astype(jnp.bfloat16).astype(jnp.float32)
+        mine = own[v, z, g].astype(jnp.bfloat16).astype(jnp.float32)
         ways[v].wait_recv()
         theirs = y_in[v].astype(jnp.float32)
         for f in range(FRB):
@@ -245,7 +264,7 @@
                 out_ref.dtype
             )
 
-    for copy in coef_out:
+    for copy in live_out:
         copy.wait_send()
     for v in range(levels):
         across[v].wait_send()
@@ -266,12 +285,6 @@
 
 def stationary(rows, cols, layers, lpanel, upanel, rowmap, colmap, blockmask, front_blocks):
     levels, _, width, depth = lpanel.shape
-    wide = upanel.shape[3]
-    select = colmap[:, 0, None, :] == jnp.arange(layers, dtype=jnp.int32)[None, :, None]
-    coef = select.astype(jnp.float32) * blockmask[:, 0, 0, None, :].astype(jnp.float32)
-    coef = jnp.broadcast_to(coef[..., None], (levels, layers, CB, width))
-    coef = coef.reshape(levels * layers, wide)
-    rm = jnp.broadcast_to(rowmap[:, 0], (levels, width))
     bf16 = jnp.bfloat16
     vmem = pl.BlockSpec(memory_space=pltpu.VMEM)
     hbm = pl.BlockSpec(memory_space=pl.ANY)
@@ -279,21 +292,22 @@
     return pl.pallas_call(
         functools.partial(kernel, rows, cols, layers, levels, width),
         out_shape=jax.ShapeDtypeStruct(front_blocks.shape, front_blocks.dtype),
-        in_specs=[vmem, hbm, vmem, vmem, hbm],
+        in_specs=[hbm, hbm, vmem, vmem, vmem, hbm],
         out_specs=vmem,
         scratch_shapes=[
+            pltpu.VMEM((levels, width, depth), bf16),
             pltpu.VMEM(upanel[:, 0].shape, bf16),
             pltpu.VMEM(front_blocks.shape, bf16),
             pltpu.VMEM((levels, width, depth), bf16),
             pltpu.VMEM((levels, rows, width, depth), bf16),
-            pltpu.VMEM((rows, levels * layers, wide), jnp.float32),
-            pltpu.VMEM((2 * levels, layers, width, width), jnp.float32),
+            pltpu.VMEM((rows, levels, CB), jnp.int32),
+            pltpu.VMEM((levels, rows, layers, width, width), jnp.float32),
             pltpu.VMEM((levels, rows, layers, width, width), bf16),
             pltpu.VMEM((levels, 2, rows, layers, width, width), bf16),
             pltpu.VMEM((levels, width, width), bf16),
             pltpu.VMEM((levels, width, width), bf16),
-            pltpu.VMEM((levels, width), jnp.int32),
-            dma((levels + 1,)),
+            pltpu.VMEM((levels, 1), jnp.int32),
+            dma((levels + 2,)),
             dma((levels,)),
             dma((levels,)),
             dma((levels, 2)),
@@ -311,7 +325,9 @@
             dma,
         ],
         compiler_params=pltpu.CompilerParams(collective_id=0, has_side_effects=True),
-    )(lpanel[:, 0], upanel[:, 0], coef, rm, front_blocks)
+    )(
+        lpanel[:, 0], upanel[:, 0], colmap[:, 0], blockmask[:, 0, 0], rowmap[:, 0], front_blocks
+    )
 
 
 def solution(mesh):

time: 93.4 us -> 74.4 us (0.80)
  Pallas kernels: 87.9 us -> 70.7 us
  other arithmetic: 1.36 us -> 0 us
    pallas_call x1, Pallas kernels: 87.9 us -> 70.7 us  [stationary(): pl.pallas_call(functools.partial(kernel, rows, cols, layers, levels, widt...]
    broadcast_in_dim x2 -> x0, local copies, waits for them, and re-layouts: 1.38 us -> none  [the longest x1 1.31 us: stationary(): rm = jnp.broadcast_to(rowmap[:, 0], (levels, width))]
    squeeze x0 -> x1, local copies, waits for them, and re-layouts: none -> 1.3 us  [stationary(): rowmap[:, 0]]
    unnamed x2 -> x1, local copies, waits for them, and re-layouts: 2.48 us -> 1.87 us
where the time goes in v2:
time: 74.4 us; the launch traced here: 73.8 us
  Pallas kernels  70.7 us (95%)
  local copies, waits for them, and re-layouts  3.16 us (4%)
    pallas_call x1, Pallas kernels, stationary(): pl.pallas_call(functools.partial(kernel, rows, cols, layers, levels, widt...  70.7 us
    unnamed x1, local copies, waits for them, and re-layouts  1.87 us

profile of v2, /device:TPU:0, one launch (start us, length us, event | category | flops | bytes accessed | tf_op | source)
XLA Modules:
  0.0 73.8 jit_solution(1040571114457886376)
XLA Ops:
  0.0 1.3 %copy.7.rm_ref = s32[2,1]{1,0:T(2,128)} copy(s32[2,1]{0,1:T(1,128)} %bitcast.9) | data formatting | bytes 16 | tf_op jit(solution)/shard_map/squeeze | solution.py:329
  1.3 70.7 %shard_map.64 = bf16[2,512,256]{2,1,0:T(8,128)(2,1)} custom-call(bf16[2,256,512]{2,1,0:T(8,128)(2,1)} %bitcast.6, bf16[2,512,1024]{2,1,0:T(8,128)(2,1)} %bitcast.5, s32[2,4]{1,0:T(2,128)} %bitcast.7, s32[2,4]{1,0:T(2,128)} %bitcast.8, s32[2,1]{1,0:T(2,128)} %copy.7.rm_ref, bf16[2,512,256]{2,1,0:T(8,128)(2,1)} %front_hbm.1), custom_call_target="tpu_custom_call" | custom-call | tf_op jit(solution)/shard_map/pallas_call | solution.py:292
  72.0 1.9 %copy.9 = bf16[2,512,256]{2,1,0:T(8,128)(2,1)} copy(bf16[2,512,256]{2,1,0:T(8,128)(2,1)} %shard_map.64) | data formatting | bytes 1048576

commit v3 on v2

--- a/solution.py
+++ b/solution.py
@@ -56,7 +56,7 @@
     rows, cols, layers, levels, width,
     l_hbm, u_hbm, cm_ref, live_ref, rm_ref, front_hbm, out_ref,
     l_ref, u_ref, front_ref, crossed, l_all, live_all, own, part, p_in, y_out, y_in, rm_in,
-    in_sem, x_send, x_recv, l_send, l_recv, loc_sem, relay_send, m_send, m_recv, m_loc,
+    in_sem, x_send, x_recv, l_send, l_recv, loc_sem, post_send, relay_send, m_send, m_recv, m_loc,
     p_send, p_recv, y_send, y_recv, rm_send, rm_recv,
 ):
     z = lax.axis_index("row")
@@ -90,33 +90,37 @@
             device_id=where, device_id_type=MESH,
         )
 
+    half = width // 2
+    pieces = [slice(h * half, (h + 1) * half) for h in range(2)]
+
     across = [
-        remote(l_ref.at[v], crossed.at[v], x_send.at[v], x_recv.at[v], {"col": far})
+        remote(l_ref.at[v, pieces[1]], crossed.at[v], x_send.at[v], x_recv.at[v], {"col": far})
         for v in range(levels)
     ]
 
-    def place(v, half):
-        k = c if half == 0 else far
-        block = l_ref.at[v] if half == 0 else crossed.at[v]
-        copy = remote(block, l_all.at[v, z], l_send.at[v, half], l_recv.at[v, z], {"row": k})
-        local = pltpu.make_async_copy(block, l_all.at[v, z], loc_sem.at[v])
-        return k, copy, local
-
-    def start_place(v, half):
-        k, copy, local = place(v, half)
-
-        @pl.when(k != z)
+    def place(v, h):
+        to = c if h == 0 else far
+        block = l_ref.at[v, pieces[0]] if h == 0 else crossed.at[v]
+        spot = l_all.at[v, z, pieces[h]]
+        copy = remote(block, spot, l_send.at[v, h], l_recv.at[v, h, z], {"row": to})
+        return to, copy, block, spot
+
+    def start_place(v, h):
+        to, copy, block, spot = place(v, h)
+
+        @pl.when(to != z)
         def _():
             copy.start()
 
-        @pl.when(k == z)
-        def _():
-            local.start()
+        @pl.when(to == z)
+        def _():
+            pltpu.make_async_copy(block, spot, loc_sem.at[v, h]).start()
 
     first.wait()
     for v in range(levels):
         across[v].start()
-    start_place(0, 0)
+    for v in range(levels):
+        start_place(v, 0)
 
     own_live = pltpu.make_async_copy(live_ref, live_all.at[z], m_loc)
     own_live.start()
@@ -132,10 +136,6 @@
 
     across[0].wait_recv()
     start_place(0, 1)
-    for v in range(1, levels):
-        start_place(v, 0)
-        across[v].wait_recv()
-        start_place(v, 1)
 
     own_live.wait()
     for step in range(1, rows):
@@ -150,38 +150,69 @@
         up = rows - 1 - near + wrap * (2 * near - rows - rows // 2 + 1)
         return low * up + (1 - low) * (rows - 1 - up)
 
-    def hop(v, a, side, to):
+    def hop(v, a, l, side, to):
         return remote(
-            part.at[v, a], p_in.at[v, side, a], p_send.at[v, a], p_recv.at[v, side, a], {"row": to}
-        )
-
+            part.at[v, a, l], p_in.at[v, side, a, l],
+            p_send.at[v, a, l], p_recv.at[v, side, a, l], {"row": to},
+        )
+
+    turns = (other, g)
     right, left = lax.rem(z + 1, rows), lax.rem(z + rows - 1, rows)
 
-    def send(v, a, side, to):
-        for l in range(layers):
-            part[v, a, l] = own[v, a, l].astype(jnp.bfloat16)
-        hop(v, a, side, to).start()
-
-    def item(v, a):
-        relay = remote(
-            l_all.at[v, a], l_all.at[v, a], relay_send.at[v, a], l_recv.at[v, a], {"col": mate}
-        )
-
-        @pl.when(gate)
-        def _():
+    def send(v, a, l, side, to):
+        part[v, a, l] = own[v, a, l].astype(jnp.bfloat16)
+        hop(v, a, l, side, to).start()
+
+    def passes(v, a, h):
+        spot = l_all.at[v, a, pieces[h]]
+        post = remote(spot, spot, post_send.at[v, a], l_recv.at[v, h, a], {"col": far})
+        relay = remote(spot, spot, relay_send.at[v, h, a], l_recv.at[v, h, a], {"col": mate})
+        return post, relay
+
+    def stage(v, a):
+        def gather(h):
+            post, relay = passes(v, a, h)
+
             @pl.when(a == z)
             def _():
-                pltpu.make_async_copy(l_ref.at[v], l_all.at[v, z], loc_sem.at[v]).wait()
+                spot = l_all.at[v, z, pieces[h]]
+                pltpu.make_async_copy(l_ref.at[v, pieces[h]], spot, loc_sem.at[v, h]).wait()
 
             @pl.when(a != z)
             def _():
                 relay.wait_recv()
 
+            post.start()
             relay.start()
 
+        def take(h):
+            _post, relay = passes(v, a, h)
+            relay.wait_recv()
+            relay.start()
+
+        @pl.when(c == z)
+        def _():
+            gather(0)
+            take(1)
+
+        @pl.when(far == z)
+        def _():
+            gather(1)
+            take(0)
+
         @pl.when(jnp.logical_not(gate))
         def _():
-            relay.wait_recv()
+            for h in range(2):
+                passes(v, a, h)[1].wait_recv()
+
+    def item(v, i):
+        a = order(i)
+        stage(v, a)
+        if v + 1 < levels:
+            @pl.when(i == 0)
+            def _():
+                across[v + 1].wait_recv()
+                start_place(v + 1, 1)
 
         block = l_all[v, a]
         for j in range(CB):
@@ -199,31 +230,45 @@
 
         @pl.when(jnp.logical_and(a > z, z == 0))
         def _():
-            send(v, a, 0, right)
+            for l in turns:
+                send(v, a, l, 0, right)
 
         @pl.when(jnp.logical_and(a < z, z == rows - 1))
         def _():
-            send(v, a, 1, left)
-
-    def collect(v, a, side):
-        hop(v, a, side, right).wait_recv()
-        for l in range(layers):
-            own[v, a, l] += p_in[v, side, a, l].astype(jnp.float32)
-
-    def forward(v, a):
+            for l in turns:
+                send(v, a, l, 1, left)
+
+    def collect(v, a, l, side):
+        hop(v, a, l, side, right).wait_recv()
+        own[v, a, l] += p_in[v, side, a, l].astype(jnp.float32)
+
+    def forward(v, i):
+        a = order(i)
+
         @pl.when(jnp.logical_and(a > z, z > 0))
         def _():
-            collect(v, a, 0)
-            send(v, a, 0, right)
+            for l in turns:
+                collect(v, a, l, 0)
+                send(v, a, l, 0, right)
 
         @pl.when(jnp.logical_and(a < z, z < rows - 1))
         def _():
-            collect(v, a, 1)
-            send(v, a, 1, left)
+            for l in turns:
+                collect(v, a, l, 1)
+                send(v, a, l, 1, left)
+
+    def finish(v, l):
+        @pl.when(z > 0)
+        def _():
+            collect(v, z, l, 0)
+
+        @pl.when(z < rows - 1)
+        def _():
+            collect(v, z, l, 1)
 
     def over_rows(step, v):
         def body(i, carry):
-            step(v, order(i))
+            step(v, i)
             return carry
 
         lax.fori_loop(0, rows, body, 0)
@@ -236,18 +281,12 @@
     for v in range(levels):
         over_rows(forward, v)
 
-        @pl.when(z > 0)
-        def _():
-            collect(v, z, 0)
-
-        @pl.when(z < rows - 1)
-        def _():
-            collect(v, z, 1)
-
+        finish(v, other)
         y_out[v] = own[v, z, other].astype(jnp.bfloat16)
         way = remote(y_out.at[v], y_in.at[v], y_send.at[v], y_recv.at[v], {"gz": other})
         way.start()
         ways.append(way)
+        finish(v, g)
 
     loads[levels].wait()
     rm_copy.wait()
@@ -269,18 +308,17 @@
     for v in range(levels):
         across[v].wait_send()
         ways[v].wait_send()
-        for half in range(2):
-            k, copy, _local = place(v, half)
-            pl.when(k != z)(copy.wait_send)
+        for h in range(2):
+            to, copy, _block, _spot = place(v, h)
+            pl.when(to != z)(copy.wait_send)
         for a in range(rows):
-            relay = remote(
-                l_all.at[v, a], l_all.at[v, a], relay_send.at[v, a], l_recv.at[v, a], {"col": mate}
-            )
-            pl.when(gate)(relay.wait_send)
-            sent = remote(
-                part.at[v, a], p_in.at[v, 0, a], p_send.at[v, a], p_recv.at[v, 0, a], {"gz": other}
-            )
-            pl.when(a != z)(sent.wait_send)
+            for h in range(2):
+                post, relay = passes(v, a, h)
+                pl.when(gate)(relay.wait_send)
+                if h == 0:
+                    pl.when(gate)(post.wait_send)
+            for l in range(layers):
+                pl.when(a != z)(hop(v, a, l, 0, right).wait_send)
 
 
 def stationary(rows, cols, layers, lpanel, upanel, rowmap, colmap, blockmask, front_blocks):
@@ -298,7 +336,7 @@
             pltpu.VMEM((levels, width, depth), bf16),
             pltpu.VMEM(upanel[:, 0].shape, bf16),
             pltpu.VMEM(front_blocks.shape, bf16),
-            pltpu.VMEM((levels, width, depth), bf16),
+            pltpu.VMEM((levels, width // 2, depth), bf16),
             pltpu.VMEM((levels, rows, width, depth), bf16),
             pltpu.VMEM((rows, levels, CB), jnp.int32),
             pltpu.VMEM((levels, rows, layers, width, width), jnp.float32),
@@ -311,14 +349,15 @@
             dma((levels,)),
             dma((levels,)),
             dma((levels, 2)),
+            dma((levels, 2, rows)),
+            dma((levels, 2)),
             dma((levels, rows)),
-            dma((levels,)),
-            dma((levels, rows)),
+            dma((levels, 2, rows)),
             dma((rows,)),
             dma((rows,)),
             dma,
-            dma((levels, rows)),
-            dma((levels, 2, rows)),
+            dma((levels, rows, layers)),
+            dma((levels, 2, rows, layers)),
             dma((levels,)),
             dma((levels,)),
             dma,

time: 74.4 us -> 86.3 us (1.16)
  the two profiles are of different devices: /device:TPU:0 before, /device:TPU:19 now
where the time goes in v3:
time: 86.3 us; the launch traced here: 86.1 us
  Pallas kernels  83 us (96%)
  local copies, waits for them, and re-layouts  3.16 us (4%)
    pallas_call x1, Pallas kernels, stationary(): pl.pallas_call(functools.partial(kernel, rows, cols, layers, levels, widt...  83 us
    unnamed x1, local copies, waits for them, and re-layouts  1.87 us

profile of v3, /device:TPU:19, one launch (start us, length us, event | category | flops | bytes accessed | tf_op | source)
XLA Modules:
  0.0 86.1 jit_solution(9673359962285714545)
XLA Ops:
  0.0 1.3 %copy.7.rm_ref = s32[2,1]{1,0:T(2,128)} copy(s32[2,1]{0,1:T(1,128)} %bitcast.9) | data formatting | bytes 16 | tf_op jit(solution)/shard_map/squeeze | solution.py:368
  1.3 83.0 %shard_map.64 = bf16[2,512,256]{2,1,0:T(8,128)(2,1)} custom-call(bf16[2,256,512]{2,1,0:T(8,128)(2,1)} %bitcast.6, bf16[2,512,1024]{2,1,0:T(8,128)(2,1)} %bitcast.5, s32[2,4]{1,0:T(2,128)} %bitcast.7, s32[2,4]{1,0:T(2,128)} %bitcast.8, s32[2,1]{1,0:T(2,128)} %copy.7.rm_ref, bf16[2,512,256]{2,1,0:T(8,128)(2,1)} %front_hbm.1), custom_call_target="tpu_custom_call" | custom-call | tf_op jit(solution)/shard_map/pallas_call | solution.py:330
  84.3 1.9 %copy.9 = bf16[2,512,256]{2,1,0:T(8,128)(2,1)} copy(bf16[2,512,256]{2,1,0:T(8,128)(2,1)} %shard_map.64) | data formatting | bytes 1048576

commit v4 on v3

--- a/solution.py
+++ b/solution.py
@@ -169,50 +169,51 @@
         relay = remote(spot, spot, relay_send.at[v, h, a], l_recv.at[v, h, a], {"col": mate})
         return post, relay
 
-    def stage(v, a):
-        def gather(h):
-            post, relay = passes(v, a, h)
-
-            @pl.when(a == z)
-            def _():
-                spot = l_all.at[v, z, pieces[h]]
-                pltpu.make_async_copy(l_ref.at[v, pieces[h]], spot, loc_sem.at[v, h]).wait()
-
-            @pl.when(a != z)
-            def _():
-                relay.wait_recv()
-
-            post.start()
-            relay.start()
-
-        def take(h):
-            _post, relay = passes(v, a, h)
+    def gather_half(v, a, h):
+        post, relay = passes(v, a, h)
+
+        @pl.when(a == z)
+        def _():
+            spot = l_all.at[v, z, pieces[h]]
+            pltpu.make_async_copy(l_ref.at[v, pieces[h]], spot, loc_sem.at[v, h]).wait()
+
+        @pl.when(a != z)
+        def _():
             relay.wait_recv()
-            relay.start()
-
-        @pl.when(c == z)
-        def _():
-            gather(0)
-            take(1)
-
-        @pl.when(far == z)
-        def _():
-            gather(1)
-            take(0)
+
+        post.start()
+        relay.start()
+
+    def take_half(v, a, h):
+        _post, relay = passes(v, a, h)
+        relay.wait_recv()
+        relay.start()
+
+    def gather(v, i):
+        a = order(i)
+        pl.when(c == z)(lambda: gather_half(v, a, 0))
+        pl.when(far == z)(lambda: gather_half(v, a, 1))
+
+    def take(v, i):
+        a = order(i)
+        pl.when(c == z)(lambda: take_half(v, a, 1))
+        pl.when(far == z)(lambda: take_half(v, a, 0))
+
+    def item(v, i):
+        a = order(i)
+
+        @pl.when(i == 0)
+        def _():
+            take(v, i)
+
+        @pl.when(i < rows - 1)
+        def _():
+            take(v, i + 1)
 
         @pl.when(jnp.logical_not(gate))
         def _():
             for h in range(2):
                 passes(v, a, h)[1].wait_recv()
-
-    def item(v, i):
-        a = order(i)
-        stage(v, a)
-        if v + 1 < levels:
-            @pl.when(i == 0)
-            def _():
-                across[v + 1].wait_recv()
-                start_place(v + 1, 1)
 
         block = l_all[v, a]
         for j in range(CB):
@@ -238,6 +239,9 @@
             for l in turns:
                 send(v, a, l, 1, left)
 
+        if v + 1 < levels:
+            gather(v + 1, i)
+
     def collect(v, a, l, side):
         hop(v, a, l, side, right).wait_recv()
         own[v, a, l] += p_in[v, side, a, l].astype(jnp.float32)
@@ -274,6 +278,11 @@
         lax.fori_loop(0, rows, body, 0)
 
     for v in range(levels):
+        if v == 0:
+            over_rows(gather, v)
+        if v + 1 < levels:
+            across[v + 1].wait_recv()
+            start_place(v + 1, 1)
         loads[v].wait()
         over_rows(item, v)
 

time: 86.3 us -> 67.6 us (0.78)
  the two profiles are of different devices: /device:TPU:19 before, /device:TPU:0 now
where the time goes in v4:
time: 67.6 us; the launch traced here: 67.4 us
  Pallas kernels  64.3 us (95%)
  local copies, waits for them, and re-layouts  3.16 us (5%)
    pallas_call x1, Pallas kernels, stationary(): pl.pallas_call(functools.partial(kernel, rows, cols, layers, levels, widt...  64.3 us
    unnamed x1, local copies, waits for them, and re-layouts  1.87 us

profile of v4, /device:TPU:0, one launch (start us, length us, event | category | flops | bytes accessed | tf_op | source)
XLA Modules:
  0.0 67.4 jit_solution(9755517779803635400)
XLA Ops:
  0.0 1.3 %copy.7.rm_ref = s32[2,1]{1,0:T(2,128)} copy(s32[2,1]{0,1:T(1,128)} %bitcast.9) | data formatting | bytes 16 | tf_op jit(solution)/shard_map/squeeze | solution.py:377
  1.3 64.3 %shard_map.64 = bf16[2,512,256]{2,1,0:T(8,128)(2,1)} custom-call(bf16[2,256,512]{2,1,0:T(8,128)(2,1)} %bitcast.6, bf16[2,512,1024]{2,1,0:T(8,128)(2,1)} %bitcast.5, s32[2,4]{1,0:T(2,128)} %bitcast.7, s32[2,4]{1,0:T(2,128)} %bitcast.8, s32[2,1]{1,0:T(2,128)} %copy.7.rm_ref, bf16[2,512,256]{2,1,0:T(8,128)(2,1)} %front_hbm.1), custom_call_target="tpu_custom_call" | custom-call | tf_op jit(solution)/shard_map/pallas_call | solution.py:339
  65.6 1.9 %copy.9 = bf16[2,512,256]{2,1,0:T(8,128)(2,1)} copy(bf16[2,512,256]{2,1,0:T(8,128)(2,1)} %shard_map.64) | data formatting | bytes 1048576
